TPU v7x, 32 devices: a whole 2x2x4 slice. The times are simulated.
32 devices in a mesh: row: 4 (over y, core), col: 8 (over z, x).
Axes of the slice: x: 2, y: 2, z: 4, core: 2. Of those that a mesh axis runs over, the one named last changes fastest.
Arguments:
- lower_inverse: float32 [4, 8, 1024, 1024], P('row', 'col'), may hold values from -1 to 2, as said below
- upper_inverse: float32 [4, 8, 1024, 1024], P('row', 'col'), may hold values from -1 to 2, as said below
- left_coupling: bfloat16 [4, 8, 512, 1024], P('row', 'col'), may hold values from -0.1875 to 0.1875
- right_pieces: float32 [8, 1024, 2048], P('col', None, 'row'), may hold values from -6 to 6
- interface_block: int32 [4, 8, 4], P('row', 'col'), may hold values from 0 to 7, all different within a row
- a_gg: float32 [4, 1024, 2048], P('row', 'col'), may hold values from -6 to 6
- panel_order: int32 [4], replicated, may hold values from 0 to 3, each once
Outputs:
- schur: float32 [4, 1024, 2048], P('row', 'col')
Inputs may be any that keep to these rules, and one draw needn't show every extreme that they name: `interface_block`: the 4 block ids of one subdomain are distinct. `panel_order`: A permutation of the column blocks. `lower_inverse`: lower triangular, diagonal between 1 and 2. `upper_inverse`: upper triangular, diagonal between 1 and 2.
All inputs are finite; a program needn't handle non-finite values.
Results may differ from a plain program's by a relative error of at most 0.0028.
Values sent between devices are 32-bit elements; how exact they have to be, the bound alone decides.
A program may use at most 128 MiB of HBM per device.

v0:
```python
import jax
import jax.numpy as jnp
from jax import lax
from jax.sharding import PartitionSpec as P


def column_order(panel_order):
    length = panel_order.shape[0]
    positions = jnp.arange(length, dtype=jnp.int32)
    hits = (panel_order[:, None] == positions[None, :]).astype(jnp.int32)
    return jnp.sum(hits * positions[:, None], axis=0)


def couple(lower_mat, upper_mat, left_mat, panel):
    halfway = jnp.dot(
        lower_mat, panel, precision=lax.Precision.HIGHEST, preferred_element_type=jnp.float32
    )
    solved = jnp.dot(
        upper_mat, halfway, precision=lax.Precision.HIGHEST, preferred_element_type=jnp.float32
    )
    solved = solved.astype(jnp.bfloat16)
    return jnp.dot(left_mat, solved, preferred_element_type=jnp.float32)


def place_rows(coupled, block_ids, block_total):
    block_count = block_ids.shape[0]
    block_rows = coupled.shape[0] // block_count
    targets = jnp.arange(block_total, dtype=jnp.int32)
    placed = (block_ids[:, None] == targets[None, :]).astype(jnp.float32)
    shaped = coupled.reshape(block_count, block_rows, coupled.shape[1])
    spread = jnp.einsum("kb,kwp->bwp", placed, shaped, precision=lax.Precision.HIGHEST)
    return spread.reshape(block_total * block_rows, coupled.shape[1])


def per_device(
    lower_inverse, upper_inverse, left_coupling, right_pieces, interface_block, a_gg, panel_order
):
    lower_mat = lower_inverse[0, 0]
    upper_mat = upper_inverse[0, 0]
    left_mat = left_coupling[0, 0]
    block_ids = interface_block[0, 0]
    row_count = lax.axis_size("row")
    coupled = couple(
        lower_mat, upper_mat, left_mat, lax.all_gather(right_pieces, "row", axis=2, tiled=True)[0]
    )
    order = column_order(panel_order)
    width_piece = right_pieces.shape[2]
    height = coupled.shape[0]
    coupled = coupled.reshape(height, row_count, width_piece)[:, order, :].reshape(
        height, row_count * width_piece
    )
    block_rows = a_gg.shape[1]
    owned = lax.psum_scatter(
        place_rows(coupled, block_ids, block_rows * lax.axis_size("col") // block_rows),
        "col",
        scatter_dimension=0,
        tiled=True,
    )
    return (a_gg[0] - owned)[None]


def solution(mesh):
    return jax.shard_map(
        per_device,
        mesh=mesh,
        in_specs=(
            P("row", "col", None, None),
            P("row", "col", None, None),
            P("row", "col", None, None),
            P("col", None, "row"),
            P("row", "col", None),
            P("row", "col", None),
            P(),
        ),
        out_specs=P("row", "col", None),
        check_vma=False,
    )
```

profile of v0, /device:TPU:0, one launch (start us, length us, event | category | flops | bytes accessed | tf_op | source)
XLA Modules:
  0.0 355.0 jit_solution(11095625044394549900)
XLA Ops:
  6.5 0.0 copy-start
  6.5 0.0 all-gather.2.cloned.1.call-start
  6.5 0.7 all-gather.2.cloned.1.call-update
  7.3 0.0 reduce-scatter.2.cloned.1.call-start
  7.3 0.7 select_reduce_fusion
  8.1 61.9 %all-gather.2.cloned.1.call-done = f32[1,1024,2048]{2,1,0:T(8,128)} async-done(((f32[1,1024,512]{2,1,0:T(8,128)}), f32[1,1024,2048]{2,1,0:T(8,128)}) %all-gather.2.cloned.1.call-update) | async-done | bytes 8388624 | tf_op jit(solution)/shard_map/all_gather | solution.py:44
  69.9 0.0 copy-start.4
  69.9 29.7 %fusion = f32[1024,2048]{1,0:T(8,128)S(1)} fusion(f32[1,1024,2048]{2,1,0:T(8,128)} %all-gather.2.cloned.1.call-done, f32[1,1,1024,1024]{3,2,1,0:T(8,128)} %param.7), kind=kOutput, calls=%fused_computation.1 | convolution fusion | flops 25769803776 | bytes 20971520 | tf_op jit(solution)/shard_map/dot_general | solution.py:15
  99.7 0.0 copy-done.4
  99.7 53.0 %fusion.2 = bf16[2048,1024]{1,0:T(8,128)(2,1)S(1)} fusion(f32[1024,2048]{1,0:T(8,128)S(1)} %fusion, f32[1,1,1024,1024]{3,2,1,0:T(8,128)S(1)} %copy-done.4), kind=kOutput, calls=%fused_computation.3 | convolution fusion | flops 25769803776 | bytes 16777216 | tf_op jit(solution)/shard_map/dot_general | solution.py:18
  152.7 0.0 copy-done
  152.7 4.4 %fusion.7 = f32[2048,512]{1,0:T(8,128)} fusion(bf16[2048,1024]{1,0:T(8,128)(2,1)S(1)} %fusion.2, bf16[1,1,512,1024]{3,2,1,0:T(8,128)(2,1)S(1)} %copy-done), kind=kOutput, calls=%fused_computation.8 | convolution fusion | flops 2147483648 | bytes 9437184 | tf_op jit(solution)/shard_map/dot_general | solution.py:22
  157.0 5.2 %copy.14 = f32[512,4,512]{2,0,1:T(8,128)} copy(f32[512,4,512]{0,2,1:T(8,128)} %bitcast.35) | data formatting | bytes 8388608 | tf_op jit(solution)/shard_map/reshape | solution.py:49
  162.3 5.0 %gather_fusion = f32[4,512,512]{2,1,0:T(8,128)} fusion(f32[512,4,512]{2,0,1:T(8,128)} %copy.14, s32[1024]{0:T(1024)S(1)} %pad_clamp_fusion), kind=kCustom, calls=%fused_computation | custom fusion | bytes 8388624 | tf_op jit(solution)/shard_map/gather | solution.py:49
  167.3 6.8 %copy.15 = f32[512,4,512]{2,1,0:T(4,128)} copy(f32[512,4,512]{2,0,1:T(8,128)} %bitcast.34) | data formatting | bytes 8388608 | tf_op jit(solution)/shard_map/gather | solution.py:49
  174.1 0.0 copy-start.3
  174.1 6.1 %reshape_reshape.3 = f32[4,128,2048]{2,1,0:T(8,128)} reshape(f32[512,4,512]{2,1,0:T(4,128)} %copy.15) | data formatting | bytes 8388608 | tf_op jit(solution)/shard_map/reshape;reshape | solution.py:30
  180.2 0.0 copy-done.3
  180.2 9.9 %fusion.5 = f32[8,128,2048]{2,0,1:T(8,128)S(1)} fusion(f32[4,128,2048]{2,1,0:T(8,128)} %reshape_reshape.3, s32[4]{0:T(128)S(1)} %bitcast.36), kind=kOutput, calls=%fused_computation.6 | convolution fusion | flops 100663328 | bytes 12582928 | tf_op jit(solution)/shard_map/kb,kwp->bwp/dot_general | solution.py:31
  190.1 8.1 %copy.17 = f32[8,128,2048]{2,1,0:T(8,128)} copy(f32[8,128,2048]{2,0,1:T(8,128)S(1)} %fusion.5) | data formatting | bytes 16777216 | tf_op jit(solution)/shard_map/kb,kwp->bwp/dot_general | solution.py:31
  198.2 0.0 copy-start.1
  198.2 0.0 copy-start.2
  198.2 0.0 reduce-scatter.2.cloned.1.call-update
  198.2 147.6 %reduce-scatter.2.cloned.1.call-done = f32[128,2048]{1,0:T(8,128)} async-done(((f32[1024,2048]{1,0:T(8,128)}), f32[128,2048]{1,0:T(8,128)}) %reduce-scatter.2.cloned.1.call-update) | async-done | bytes 1048592 | tf_op jit(solution)/shard_map/reduce_scatter | solution.py:53
  345.8 0.0 copy-done.2
  345.8 2.3 fusion.10
  348.1 0.0 copy-done.1
  (2 shorter events, 0.0 us)
Async XLA Ops:
  6.5 146.1 %copy-start = (bf16[1,1,512,1024]{3,2,1,0:T(8,128)(2,1)S(1)}, bf16[1,1,512,1024]{3,2,1,0:T(8,128)(2,1)}, u32[]{:S(2)}) copy-start(bf16[1,1,512,1024]{3,2,1,0:T(8,128)(2,1)} %param.9) | copy-start | bytes 3145732
  6.5 63.4 %all-gather.2.cloned.1.call-start = ((), (), s32[]{:S(2)}) async-start(), calls=%async_computation.1 | async-start | bytes 10485760 | tf_op jit(solution)/shard_map/all_gather | solution.py:44
  7.3 338.5 %reduce-scatter.2.cloned.1.call-start = ((), (), s32[]{:S(2)}) async-start(), calls=%async_computation.2 | async-start | bytes 9437184 | tf_op jit(solution)/shard_map/reduce_scatter | solution.py:53
  69.9 29.8 %copy-start.4 = (f32[1,1,1024,1024]{3,2,1,0:T(8,128)S(1)}, f32[1,1,1024,1024]{3,2,1,0:T(8,128)}, u32[]{:S(2)}) copy-start(f32[1,1,1024,1024]{3,2,1,0:T(8,128)} %param.8) | copy-start | bytes 12582916
  174.1 6.1 %copy-start.3 = (s32[1,1,4]{2,1,0:T(1,128)S(1)}, s32[1,1,4]{2,1,0:T(1,128)}, u32[]{:S(2)}) copy-start(s32[1,1,4]{2,1,0:T(1,128)} %param.11) | copy-start | bytes 52
  198.2 149.9 %copy-start.1 = (bf16[1,1,512,1024]{3,2,1,0:T(8,128)(2,1)S(1)}, bf16[1,1,512,1024]{3,2,1,0:T(8,128)(2,1)}, u32[]{:S(2)}) copy-start(bf16[1,1,512,1024]{3,2,1,0:T(8,128)(2,1)} %param.9) | copy-start | bytes 3145732
  198.2 147.6 %copy-start.2 = (f32[1,128,2048]{2,1,0:T(8,128)S(1)}, f32[1,128,2048]{2,1,0:T(8,128)}, u32[]{:S(2)}) copy-start(f32[1,128,2048]{2,1,0:T(8,128)} %param.12) | copy-start | bytes 3145732
Sparse Core Ops, SparseCore 0:
  8.9 60.9 all-gather.1
  198.3 147.4 reduce-scatter.1
where the time goes:
time: 355 us
  waiting for transfers between devices  210 us (59%)
  matrix products  97 us (27%)
  local copies, waits for them, and re-layouts  31.2 us (9%)
  between operations  13.4 us (4%)
    reduce_scatter x1, waiting for transfers between devices, per_device(): lax.psum_scatter(place_rows(coupled, block_ids, block_rows * lax.axis_siz...  148 us
    all_gather x1, waiting for transfers between devices, per_device(): lax.all_gather(right_pieces, 'row', axis=2, tiled=True)[0]  61.9 us
    dot_general x1, matrix products, couple(): jnp.dot(upper_mat, halfway, precision=lax.Precision.HIGHEST, preferred_el...  53 us
    dot_general x1, matrix products, couple(): jnp.dot(lower_mat, panel, precision=lax.Precision.HIGHEST, preferred_elem...  29.7 us
    gather x2, local copies, waits for them, and re-layouts, per_device(): coupled.reshape(height, row_count, width_piece)[:, order, :]  11.8 us
    dot_general x1, matrix products, place_rows(): jnp.einsum('kb,kwp->bwp', placed, shaped, precision=lax.Precision.HIGHEST)  9.92 us
    dot_general x1, local copies, waits for them, and re-layouts, place_rows(): jnp.einsum('kb,kwp->bwp', placed, shaped, precision=lax.Precision.HIGHEST)  8.08 us
  transfers between devices with their start and end apart: 2, of which 2 were waited for; matrix products, arithmetic and copies ran while one was open for 0% of the time, Pallas kernels for 0%

commit v1 on v0

v1 whole, which is shorter than its diff:
```python
import functools

import jax
import jax.numpy as jnp
import numpy as np
from jax import lax
from jax.experimental import pallas as pl
from jax.experimental.pallas import tpu as pltpu
from jax.sharding import PartitionSpec as P

MESH = pl.DeviceIdType.MESH
GROUP_WIDTH = 512
TILE = 256
VMEM_LIMIT = 60 * 1024 * 1024


def ring_order(length):
    return list(range(0, length, 2)) + list(range(1, length, 2))[::-1]


def ring_neighbours(col, count):
    odd = lax.rem(col, 2)
    even_next = col + 2 - (col + 2) // count
    odd_next = col - 2 + (count - col) // (count - 1)
    even_prev = col - 2 + 3 * ((count - col) // count)
    odd_prev = col + 2 - 3 * ((col + 1) // count)
    return (1 - odd) * even_next + odd * odd_next, (1 - odd) * even_prev + odd * odd_prev


def split(value):
    high = value.astype(jnp.bfloat16)
    return high, (value - high.astype(jnp.float32)).astype(jnp.bfloat16)


def kernel(
    row_count, col_count, groups,
    lower_ref, upper_ref, left_ref, piece_ref, out_ref,
    panel, lower_high, lower_low, upper_high, upper_low,
    x_high, x_low, half_high, half_low, solved, coupled, sums,
    gather_send, gather_recv, ring_send, ring_recv,
):
    row = lax.axis_index("row")
    col = lax.axis_index("col")
    ahead, behind = ring_neighbours(col, col_count)
    inner, width = piece_ref.shape
    rows = left_ref.shape[0] // col_count
    half = coupled.shape[2] // 2

    def swapped(bit):
        return (row + bit * (1 - 2 * lax.rem(row // bit, 2)), col)

    bits = []
    bit = row_count // 2
    while bit >= 1:
        bits.append(bit)
        bit //= 2
    targets = ((row, ahead), (row, behind))
    barrier = pltpu.get_barrier_semaphore()
    partners = [swapped(b) for b in bits] + list(targets)
    for partner in partners:
        pl.semaphore_signal(barrier, inc=1, device_id=partner, device_id_type=MESH)
    pl.semaphore_wait(barrier, len(partners))

    def held(mask):
        return piece_ref if mask == 0 else panel.at[mask - 1]

    def gather(mask):
        low = mask & -mask
        return pltpu.make_async_remote_copy(
            src_ref=held(mask ^ low), dst_ref=panel.at[mask - 1],
            send_sem=gather_send.at[mask - 1], recv_sem=gather_recv.at[mask - 1],
            device_id=swapped(low), device_id_type=MESH,
        )

    def pass_on(mask):
        for b in bits:
            if mask == 0 or b < (mask & -mask):
                gather(mask | b).start()

    def ring(group, side, step):
        if step == 0:
            slot = 0 if side == 0 else col_count - 2
            src = coupled.at[group, pl.ds(slot * rows, rows), pl.ds(side * half, half)]
        else:
            src = sums.at[group, side, step - 1]
        return pltpu.make_async_remote_copy(
            src_ref=src, dst_ref=sums.at[group, side, step],
            send_sem=ring_send.at[group, side, step], recv_sem=ring_recv.at[group, side, step],
            device_id=targets[side], device_id_type=MESH,
        )

    def begin(group):
        for side in range(2):
            ring(group, side, 0).start()

    def advance(group, step):
        last = step == col_count - 1
        for side in range(2):
            ring(group, side, step - 1).wait_recv()
            slot = step if last or side == 0 else col_count - 2 - step
            own = coupled[group, slot * rows:(slot + 1) * rows, side * half:(side + 1) * half]
            total = sums[group, side, step - 1] + own
            if last:
                at = group * 2 * half + side * half
                out_ref[:, at:at + half] = total
            else:
                sums[group, side, step - 1] = total
                ring(group, side, step).start()

    def tiles(count, body):
        def one(i, carry):
            body(pl.ds(pl.multiple_of(i * TILE, TILE), TILE))
            return carry

        lax.fori_loop(0, count // TILE, one, 0)

    def dot(a, b):
        return jnp.dot(a, b, preferred_element_type=jnp.float32)

    def three(a_high, a_low, b_high, b_low, at):
        high = a_high[at, :]
        return dot(high, b_high[...]) + (dot(high, b_low[...]) + dot(a_low[at, :], b_high[...]))

    def compute(group):
        for place, mask in enumerate(groups[group]):
            if mask:
                gather(mask).wait_recv()
                pass_on(mask)
        cols = [slice(place * width, (place + 1) * width) for place in range(len(groups[group]))]

        def cut(at):
            for place, mask in enumerate(groups[group]):
                high, low = split(held(mask)[at, :])
                x_high[at, cols[place]] = high
                x_low[at, cols[place]] = low

        tiles(inner, cut)

        def first(at):
            high, low = split(three(lower_high, lower_low, x_high, x_low, at))
            half_high[at, :] = high
            half_low[at, :] = low

        tiles(inner, first)

        def second(at):
            solved[at, :] = three(upper_high, upper_low, half_high, half_low, at).astype(jnp.bfloat16)

        tiles(inner, second)

        def third(at):
            coupled[group, at, :] = dot(left_ref[at, :], solved[...])

        tiles(left_ref.shape[0], third)

    pass_on(0)

    def factors(at):
        lower_high[at, :], lower_low[at, :] = split(lower_ref[at, :])
        upper_high[at, :], upper_low[at, :] = split(upper_ref[at, :])

    tiles(inner, factors)

    near = (len(groups) + 1) // 2
    done = {}
    for group in range(len(groups)):
        if group >= near:
            steps = col_count - 3 if group == near else col_count - 1
            for step in range(1, steps + 1):
                for other in range(near):
                    if done[other] < step:
                        advance(other, step)
                        done[other] = step
        compute(group)
        begin(group)
        done[group] = 0
    for step in range(1, col_count):
        for group in range(len(groups)):
            if done[group] < step:
                advance(group, step)
    for mask in range(1, row_count):
        gather(mask).wait_send()
    for group in range(len(groups)):
        for side in range(2):
            for step in range(col_count - 1):
                ring(group, side, step).wait_send()


def gather_solve_sum(lower_mat, upper_mat, left_mat, piece):
    row_count = lax.axis_size("row")
    col_count = lax.axis_size("col")
    inner, width = piece.shape
    per = max(1, GROUP_WIDTH // width)
    groups = [list(range(at, min(at + per, row_count))) for at in range(0, row_count, per)]
    wide = per * width
    count = len(groups)
    rows = left_mat.shape[0] // col_count
    bf16, f32 = jnp.bfloat16, jnp.float32
    dma = pltpu.SemaphoreType.DMA
    return pl.pallas_call(
        functools.partial(kernel, row_count, col_count, groups),
        out_shape=jax.ShapeDtypeStruct((rows, row_count * width), f32),
        in_specs=[pl.BlockSpec(memory_space=pltpu.VMEM)] * 4,
        out_specs=pl.BlockSpec(memory_space=pltpu.VMEM),
        scratch_shapes=[
            pltpu.VMEM((row_count - 1, inner, width), f32),
            pltpu.VMEM((inner, inner), bf16),
            pltpu.VMEM((inner, inner), bf16),
            pltpu.VMEM((inner, inner), bf16),
            pltpu.VMEM((inner, inner), bf16),
            pltpu.VMEM((inner, wide), bf16),
            pltpu.VMEM((inner, wide), bf16),
            pltpu.VMEM((inner, wide), bf16),
            pltpu.VMEM((inner, wide), bf16),
            pltpu.VMEM((inner, wide), bf16),
            pltpu.VMEM((count, left_mat.shape[0], wide), f32),
            pltpu.VMEM((count, 2, col_count - 1, rows, wide // 2), f32),
            dma((row_count - 1,)),
            dma((row_count - 1,)),
            dma((count, 2, col_count - 1)),
            dma((count, 2, col_count - 1)),
        ],
        compiler_params=pltpu.CompilerParams(
            collective_id=0, has_side_effects=True, vmem_limit_bytes=VMEM_LIMIT
        ),
    )(lower_mat, upper_mat, left_mat, piece)


def ring_rows(left_mat, block_ids, owners):
    block_count = block_ids.shape[0]
    shaped = left_mat.reshape(block_count, left_mat.shape[0] // block_count, left_mat.shape[1])
    placed = jnp.zeros((owners.shape[0],) + shaped.shape[1:], left_mat.dtype)
    for k in range(block_count):
        hit = (owners == block_ids[k])[:, None, None]
        placed = jnp.where(hit, shaped[k][None], placed)
    return placed.reshape(-1, left_mat.shape[1])


def per_device(
    lower_inverse, upper_inverse, left_coupling, right_pieces, interface_block, a_gg, panel_order
):
    row_count = lax.axis_size("row")
    col_count = lax.axis_size("col")
    order = ring_order(col_count)
    table = np.zeros((col_count, col_count), np.int32)
    for place, col in enumerate(order):
        for u in range(col_count):
            table[col, u] = order[(place - 1 - u) % col_count]
    owners = jnp.asarray(table)[lax.axis_index("col")]
    left_mat = ring_rows(left_coupling[0, 0], interface_block[0, 0], owners)
    width = right_pieces.shape[2]
    base = a_gg[0]
    total = gather_solve_sum(lower_inverse[0, 0], upper_inverse[0, 0], left_mat, right_pieces[0])
    me = lax.axis_index("row")
    positions = jnp.arange(row_count, dtype=jnp.int32)
    stored = jnp.sum((panel_order[:, None] == positions[None, :]).astype(jnp.int32) * positions[:, None], axis=0)
    stored = jnp.bitwise_xor(stored, me.astype(jnp.int32))
    columns = [
        base[:, b * width:(b + 1) * width]
        - lax.dynamic_slice(total, (0, stored[b] * width), (total.shape[0], width))
        for b in range(row_count)
    ]
    return jnp.concatenate(columns, axis=1)[None]


def solution(mesh):
    return jax.shard_map(
        per_device,
        mesh=mesh,
        in_specs=(
            P("row", "col", None, None),
            P("row", "col", None, None),
            P("row", "col", None, None),
            P("col", None, "row"),
            P("row", "col", None),
            P("row", "col", None),
            P(),
        ),
        out_specs=P("row", "col", None),
        check_vma=False,
    )
```

time: 355 us -> 140 us (0.39)
  waiting for transfers between devices: 210 us -> 0 us
  Pallas kernels: 0 us -> 126 us
  matrix products: 97 us -> 0 us
  local copies, waits for them, and re-layouts: 31.2 us -> 3.57 us
  between operations: 13.4 us -> 2.64 us
  other arithmetic: 3.06 us -> 8.03 us
    reduce_scatter x1 -> x0, waiting for transfers between devices: 148 us -> none  [per_device(): lax.psum_scatter(place_rows(coupled, block_ids, block_rows * lax.axis_siz...]
    pallas_call x0 -> x1, Pallas kernels: none -> 126 us  [gather_solve_sum(): pl.pallas_call(functools.partial(kernel, row_count, col_count, groups), o...]
    dot_general x4 -> x0, matrix products: 97 us -> none  [the longest x1 53 us: couple(): jnp.dot(upper_mat, halfway, precision=lax.Precision.HIGHEST, preferred_el...]
    all_gather x1 -> x0, waiting for transfers between devices: 61.9 us -> none  [per_device(): lax.all_gather(right_pieces, 'row', axis=2, tiled=True)[0]]
    gather x2 -> x0, local copies, waits for them, and re-layouts: 11.8 us -> none  [per_device(): coupled.reshape(height, row_count, width_piece)[:, order, :]]
    dot_general x1 -> x0, local copies, waits for them, and re-layouts: 8.08 us -> none  [place_rows(): jnp.einsum('kb,kwp->bwp', placed, shaped, precision=lax.Precision.HIGHEST)]
    another operation x1 -> x0, local copies, waits for them, and re-layouts: 6.09 us -> none  [place_rows(): shaped = coupled.reshape(block_count, block_rows, coupled.shape[1])]
    reshape x1 -> x0, local copies, waits for them, and re-layouts: 5.23 us -> none  [per_device(): coupled.reshape(height, row_count, width_piece)[:, order, :]]
  transfers between devices with their start and end apart: 2 -> 0, of which waited for: 2 -> 0; matrix products, arithmetic and copies ran while one was open for 0% -> 0% of each run, Pallas kernels for 0% -> 0%
where the time goes in v1:
time: 140 us
  Pallas kernels  126 us (90%)
  other arithmetic  8.03 us (6%)
  local copies, waits for them, and re-layouts  3.57 us (3%)
  between operations  2.64 us (2%)
    pallas_call x1, Pallas kernels, gather_solve_sum(): pl.pallas_call(functools.partial(kernel, row_count, col_count, groups), o...  126 us
    eq x1, other arithmetic, ring_rows(): hit = (owners == block_ids[k])[:, None, None]  3.27 us

profile of v1, /device:TPU:0, one launch (start us, length us, event | category | flops | bytes accessed | tf_op | source)
XLA Modules:
  0.0 140.0 jit_solution(8897538301439358264)
XLA Ops:
  0.0 1.5 %fusion.4 = (s32[1,1,1]{2,1,0:T(1,128)}, s32[1,1,1]{2,1,0:T(1,128)}, s32[1,1,1]{2,1,0:T(1,128)}, s32[1,1,1]{2,1,0:T(1,128)}) fusion(s32[1,1,4]{2,1,0:T(1,128)} %param.12), kind=kLoop, calls=%fused_computation.26 | loop fusion | bytes 32 | tf_op jit(solution)/shard_map/slice | solution.py:234
  1.5 3.3 %compare_bitcast_fusion.3 = (pred[8]{0:T(512)(128)(4,1)S(1)}, pred[8]{0:T(512)(128)(4,1)S(1)}, pred[8]{0:T(512)(128)(4,1)S(1)}, pred[8]{0:T(512)(128)(4,1)S(1)}) fusion(s32[]{:T(128)} %bitcast.3, s32[8,8]{1,0:T(8,128)} %constant.25.clone, s32[]{:T(128)S(6)} %select_n.32, s32[]{:T(128)} %bitcast.8, s32[]{:T(128)} %bitcast.13, s32[]{:T(128)} %bitcast.18), kind=kLoop, calls=%fused_computation.18 | loop fusion | flops 32 | bytes 84 | tf_op jit(solution)/shard_map/eq | solution.py:234
  4.7 0.1 broadcast_bitcast_fusion.2
  4.8 0.1 broadcast_bitcast_fusion
  4.9 1.3 slice_bitcast_fusion.3
  6.2 2.2 %fusion.2.left_ref = bf16[1024,1024]{1,0:T(8,128)(2,1)} fusion(pred[1024]{0:T(1024)(128)(4,1)S(1)} %get-tuple-element.25, pred[1024]{0:T(1024)(128)(4,1)S(1)} %get-tuple-element.26, pred[1024]{0:T(1024)(128)(4,1)S(1)} %get-tuple-element.27, pred[1024]{0:T(1024)(128)(4,1)S(1)} %get-tuple-element.28, bf16[128,1024]{1,0:T(8,128)(2,1)S(1)} %get-tuple-element.11, ...), kind=kLoop, calls=%fused_computation.3 | loop fusion | flops 4194304 | bytes 3149824 | tf_op jit(solution)/shard_map/jit(_where)/select_n | solution.py:235
  8.4 0.0 copy-start.1
  8.4 0.0 copy-start
  8.4 125.8 %shard_map.82 = f32[128,2048]{1,0:T(8,128)} custom-call(f32[1024,1024]{1,0:T(8,128)} %bitcast.52, f32[1024,1024]{1,0:T(8,128)} %bitcast.53, bf16[1024,1024]{1,0:T(8,128)(2,1)} %fusion.2.left_ref, f32[1024,512]{1,0:T(8,128)} %bitcast.54), custom_call_target="tpu_custom_call" | custom-call | tf_op jit(solution)/shard_map/pallas_call | solution.py:200
  134.2 0.0 copy-done.1
  134.2 0.1 select_reduce_fusion
  134.3 0.7 fusion.3
  137.6 0.0 copy-done
  137.6 1.4 %slice_subtract_fusion.3 = (f32[128,512]{1,0:T(8,128)S(1)}, f32[128,512]{1,0:T(8,128)S(1)}, f32[128,512]{1,0:T(8,128)S(1)}, f32[128,512]{1,0:T(8,128)S(1)}) fusion(f32[128,2048]{1,0:T(8,128)S(1)} %bitcast.55, f32[128,2048]{1,0:T(8,128)} %shard_map.82, s32[]{:T(128)S(6)} %select_n.37, s32[]{:T(128)S(6)} %select_n.40, s32[]{:T(128)S(6)} %select_n.39, ...), kind=kLoop, calls=%fused_computation.8 | loop fusion | flops 262144 | bytes 3145744 | tf_op jit(solution)/shard_map/sub | solution.py:259
  139.0 1.0 maximum_bitcast_fusion
  (1 shorter events, 0.0 us)
Async XLA Ops:
  8.4 125.8 %copy-start.1 = (s32[4]{0:T(128)S(1)}, s32[4]{0:T(128)}, u32[]{:S(2)}) copy-start(s32[4]{0:T(128)} %param.14) | copy-start | bytes 52
  8.4 129.2 %copy-start = (f32[1,128,2048]{2,1,0:T(8,128)S(1)}, f32[1,128,2048]{2,1,0:T(8,128)}, u32[]{:S(2)}) copy-start(f32[1,128,2048]{2,1,0:T(8,128)} %param.13) | copy-start | bytes 3145732
